TPU v7x, 32 devices: a whole 2x2x4 slice. The times are simulated.
32 devices in a mesh: rad: 8 (over y, x, core), ang: 4 (over z).
Axes of the slice: x: 2, y: 2, z: 4, core: 2. Of those that a mesh axis runs over, the one named last changes fastest.
Arguments:
- density: float32 [3, 512, 128, 512], P(None, 'rad', 'ang'), may hold values from -13 to 13
Outputs:
- potential: float32 [3, 512, 128, 512], P(None, 'rad', 'ang')
All inputs are finite; a program needn't handle non-finite values.
Results may differ from a plain program's by a relative error of at most 0.0003.
Values sent between devices are 32-bit elements; how exact they have to be, the bound alone decides.
A program may use at most 128 MiB of HBM per device.

v0:
```python
import math
import jax
import jax.numpy as jnp
import numpy as np
from jax import lax
from jax.sharding import PartitionSpec as P

LMAX = 12
INNER = 0.5
COUPLING = 2000.0


def entering(part, axis, combine, identity, reverse):
    count = lax.axis_size(axis)
    place = lax.axis_index(axis)
    ahead = count - 1 - place if reverse else place
    gathered = lax.all_gather(part, axis)
    state = jnp.zeros_like(part) + jnp.asarray(identity, part.dtype)

    def one(turn, state):
        source = count - 1 - turn if reverse else turn
        return combine(state, lax.dynamic_index_in_dim(gathered, source, 0, False))

    return lax.fori_loop(0, ahead, one, state)


def legendre_table(polar_angle):
    cos_theta = jnp.cos(polar_angle)
    sine_theta = jnp.sin(polar_angle)
    values_lm = {}
    values_lm[0, 0] = jnp.full_like(polar_angle, 1.0 / math.sqrt(4.0 * math.pi))
    for m in range(1, LMAX + 1):
        values_lm[m, m] = (
            math.sqrt((2.0 * m + 1.0) / (2.0 * m)) * sine_theta * values_lm[m - 1, m - 1]
        )
    for m in range(0, LMAX):
        values_lm[m + 1, m] = math.sqrt(2.0 * m + 3.0) * cos_theta * values_lm[m, m]
    for m in range(0, LMAX + 1):
        for l in range(m + 2, LMAX + 1):
            coef_a = math.sqrt((4.0 * l * l - 1.0) / (l * l - m * m))
            coef_b = math.sqrt(((l - 1.0) ** 2 - m * m) / (4.0 * (l - 1.0) ** 2 - 1.0))
            values_lm[l, m] = coef_a * (
                cos_theta * values_lm[l - 1, m] - coef_b * values_lm[l - 2, m]
            )
    degree_rows = []
    for l in range(LMAX + 1):
        columns = []
        for k in range(2 * LMAX + 1):
            m = (k + 1) // 2
            columns.append(values_lm[l, m] if m <= l else jnp.zeros_like(polar_angle))
        degree_rows.append(jnp.stack(columns, -1))
    return jnp.stack(degree_rows, 1)


def fourier_table(phi_cells):
    azimuth = jnp.arange(phi_cells, dtype=jnp.float32) * (2.0 * math.pi / phi_cells)
    column = jnp.arange(2 * LMAX + 1)
    order_m = ((column + 1) // 2).astype(jnp.float32)
    phase = azimuth[:, None] * order_m[None, :]
    root_two = math.sqrt(2.0)
    return jnp.where(
        column[None, :] == 0,
        jnp.ones_like(phase),
        jnp.where(column[None, :] % 2 == 1, root_two * jnp.cos(phase), root_two * jnp.sin(phase)),
    )


def slot_selector():
    width = 2 * LMAX + 1
    used = [l * width + k for l in range(LMAX + 1) for k in range(width) if (k + 1) // 2 <= l]
    table = np.zeros(((LMAX + 1) * width, len(used)), np.float32)
    table[np.array(used), np.arange(len(used))] = 1.0
    return jnp.asarray(table)


def add_terms(earlier, later):
    return jax.tree.map(jnp.add, earlier, later)


def body(density):
    snapshots, shells, theta_rows, phi_cells = density.shape
    width = 2 * LMAX + 1
    total_shells = shells * lax.axis_size("rad")
    total_rows = theta_rows * lax.axis_size("ang")
    row_index = lax.axis_index("ang") * theta_rows + jnp.arange(theta_rows, dtype=jnp.int32)
    polar_angle = (row_index.astype(jnp.float32) + 0.5) * (math.pi / total_rows)
    legendre = legendre_table(polar_angle)
    weights = jnp.sin(polar_angle) * (math.pi / total_rows) * (2.0 * math.pi / phi_cells)
    fourier = fourier_table(phi_cells)
    spacing = (1.0 - INNER) / total_shells
    shell_index = lax.axis_index("rad") * shells + jnp.arange(shells, dtype=jnp.int32)
    radius = INNER + (shell_index.astype(jnp.float32) + 0.5) * spacing
    azimuthal = jnp.dot(
        density.reshape(snapshots * shells * theta_rows, phi_cells),
        fourier,
        precision=lax.Precision.HIGHEST,
        preferred_element_type=jnp.float32,
    )
    azimuthal = azimuthal.reshape(snapshots, shells, theta_rows, width)
    partial_moments = jnp.einsum(
        "frtk,tlk->frlk",
        azimuthal,
        legendre * weights[:, None, None],
        precision=lax.Precision.HIGHEST,
    )
    selector = slot_selector()
    packed = jnp.dot(
        partial_moments.reshape(snapshots * shells, (LMAX + 1) * width),
        selector,
        precision=lax.Precision.HIGHEST,
        preferred_element_type=jnp.float32,
    )
    summed = lax.psum(packed, "ang")
    moments = jnp.dot(
        summed, selector.T, precision=lax.Precision.HIGHEST, preferred_element_type=jnp.float32
    ).reshape(snapshots, shells, LMAX + 1, width)
    degree = jnp.arange(LMAX + 1, dtype=jnp.float32)
    inner_terms = moments * (radius[:, None] ** (degree + 2.0) * spacing)[None, :, :, None]
    outer_terms = moments * (radius[:, None] ** (1.0 - degree) * spacing)[None, :, :, None]
    inner_total = jnp.sum(inner_terms, 1)
    outer_total = jnp.sum(outer_terms, 1)
    zeros_block = jnp.zeros_like(inner_total)
    from_below = entering(inner_total, "rad", add_terms, zeros_block, False)
    from_above = entering(outer_total, "rad", add_terms, zeros_block, True)
    inner_sum = from_below[:, None] + jnp.cumsum(inner_terms, 1) - 0.5 * inner_terms
    outer_sum = (
        from_above[:, None]
        + jnp.flip(jnp.cumsum(jnp.flip(outer_terms, 1), 1), 1)
        - 0.5 * outer_terms
    )
    factor = (-COUPLING * 4.0 * math.pi / (2.0 * degree + 1.0))[None, None, :, None]
    coefficient = factor * (
        (radius[:, None] ** (-(degree[None, :] + 1.0)))[None, :, :, None] * inner_sum
        + (radius[:, None] ** degree[None, :])[None, :, :, None] * outer_sum
    )
    spread = jnp.einsum("frlk,tlk->frtk", coefficient, legendre, precision=lax.Precision.HIGHEST)
    potential = jnp.dot(
        spread.reshape(snapshots * shells * theta_rows, width),
        fourier.T,
        precision=lax.Precision.HIGHEST,
        preferred_element_type=jnp.float32,
    )
    return potential.reshape(snapshots, shells, theta_rows, phi_cells)


def solution(mesh):
    return jax.shard_map(
        body,
        mesh=mesh,
        in_specs=(P(None, "rad", "ang", None),),
        out_specs=P(None, "rad", "ang", None),
        check_vma=False,
    )
```

profile of v0, /device:TPU:0, one launch (start us, length us, event | category | flops | bytes accessed | tf_op | source)
XLA Modules:
  0.0 137.9 jit_solution(15535400083472716511)
XLA Ops:
  6.5 0.6 sine_multiply_fusion
  7.2 0.1 broadcast_multiply_fusion.4
  7.2 0.1 subtract_multiply_fusion.12
  7.3 0.1 subtract_multiply_fusion.2
  7.8 0.1 subtract_multiply_fusion.10
  7.9 0.1 broadcast_multiply_fusion.6
  8.0 0.1 subtract_multiply_fusion.4
  8.1 0.1 broadcast_multiply_fusion.28
  8.2 0.1 broadcast_multiply_fusion.12
  8.3 0.1 subtract_multiply_fusion.6
  8.7 0.1 subtract_multiply_fusion.8
  8.9 0.1 broadcast_multiply_fusion.30
  9.0 0.1 broadcast_multiply_fusion.8
  9.2 0.1 subtract_multiply_fusion.20
  9.2 0.1 subtract_multiply_fusion.18
  9.3 0.1 broadcast_multiply_fusion.14
  9.4 0.1 broadcast_multiply_fusion.24
  9.5 0.1 broadcast_multiply_fusion.16
  9.5 0.1 subtract_multiply_fusion.16
  9.6 0.1 subtract_multiply_fusion.14
  9.7 0.1 broadcast_multiply_fusion.22
  10.2 0.1 stack.72
  10.3 0.2 stack.70
  10.5 0.2 stack.68
  10.7 0.2 stack.66
  10.9 0.1 stack.64
  11.0 0.2 stack.62
  11.3 0.2 stack.60
  11.6 0.2 stack.58
  11.8 0.2 stack.56
  12.0 0.2 stack.54
  12.3 0.2 stack.50
  12.6 0.2 stack.52
  12.8 15.4 %convolution_bitcast_fusion = f32[6144,25]{0,1:T(8,128)S(1)} fusion(f32[6144,512]{1,0:T(8,128)} %bitcast.64, f32[25]{0:T(128)S(1)} %fusion.29, f32[512]{0:T(512)S(1)} %iota_multiply_fusion, pred[25]{0:T(512)(128)(4,1)S(1)} %get-tuple-element.109, pred[25]{0:T(512)(128)(4,1)S(1)} %get-tuple-element.110), kind=kOutput, calls=%fused_computation.2 | convolution fusion | flops 943782400 | bytes 13199510 | tf_op jit(solution)/shard_map/dot_general | solution.py:93
  28.2 0.8 reshape.1258
  29.0 1.0 stack.74
  30.0 5.8 %convolution_bitcast_fusion.2 = f32[3,64,13,25]{1,2,0,3:T(8,128)S(1)} fusion(f32[3,64,32,25]{2,1,0,3:T(8,128)S(1)} %reshape.1258, f32[32,13,25]{0,1,2:T(8,128)S(1)} %stack.74, f32[32]{0:T(128)} %sine_multiply_fusion), kind=kOutput, calls=%fused_computation.8 | convolution fusion | flops 23972000 | bytes 905728 | tf_op jit(solution)/shard_map/frtk,tlk->frlk/dot_general | solution.py:100
  35.8 0.3 copy.31
  36.1 0.4 reshape.1259
  36.5 0.3 copy-done
  36.8 1.5 %fusion.37 = f32[192,169]{0,1:T(8,128)} fusion(f32[192,325]{0,1:T(8,128)S(1)} %reshape.1259, f32[325,169]{1,0:T(8,128)S(1)} %copy-done), kind=kOutput, calls=%fused_computation.198 | convolution fusion | flops 126547200 | bytes 599092 | tf_op jit(solution)/shard_map/dot_general | solution.py:107
  38.3 0.2 broadcast_power_fusion
  38.6 37.2 %all-reduce.2.cloned.1.call-done = f32[192,169]{0,1:T(8,128)} async-done(((f32[192,169]{0,1:T(8,128)}), f32[192,169]{0,1:T(8,128)}) %all-reduce.2.cloned.1.call-update) | async-done | bytes 129808 | tf_op jit(solution)/shard_map/psum | solution.py:113
  75.8 1.4 fusion.38
  77.2 0.2 reshape.1260
  77.4 0.7 copy.33
  78.1 0.4 multiply_reduce_fusion
  78.6 10.2 %all-gather = f32[24,13,25]{2,1,0:T(8,128)} all-gather(f32[3,13,25]{2,1,0:T(8,128)S(1)} %get-tuple-element.86), channel_id=2, replica_groups=mesh['rad'=8,'ang'=4] {'rad'}, dimensions={0}, use_global_device_ids=true | all-gather | bytes 35100 | tf_op jit(solution)/shard_map/all_gather | solution.py:17
  88.8 14.3 %all-gather.1 = f32[24,13,25]{2,1,0:T(8,128)} all-gather(f32[3,13,25]{2,1,0:T(8,128)S(1)} %get-tuple-element.87), channel_id=3, replica_groups=mesh['rad'=8,'ang'=4] {'rad'}, dimensions={0}, use_global_device_ids=true | all-gather | bytes 35100 | tf_op jit(solution)/shard_map/all_gather | solution.py:17
  103.1 5.2 %while.23 = (s32[]{:T(128)}, f32[3,13,25]{2,1,0:T(8,128)S(1)}, s32[]{:T(128)}, f32[8,3,13,25]{3,2,1,0:T(8,128)}, s32[]{:T(128)}, /*index=5*/s32[]{:T(128)}, s32[]{:T(128)}, s32[]{:T(128)}) while((s32[]{:T(128)}, f32[3,13,25]{2,1,0:T(8,128)S(1)}, s32[]{:T(128)}, f32[8,3,13,25]{3,2,1,0:T(8,128)}, s32[]{:T(128)}, /*index=5*/s32[]{:T(128)}, ...), condition=%wide.region_7.8_spmd, body=%wide.region_6.7_spmd.sunk | while | flops 981 | bytes 11843 | solution.py:24
  103.1 0.7 bitcast_add_fusion.5
  103.8 0.7 bitcast_add_fusion.5
  104.6 0.7 bitcast_add_fusion.5
  105.3 0.7 bitcast_add_fusion.5
  106.1 0.7 bitcast_add_fusion.5
  106.8 0.7 bitcast_add_fusion.5
  107.5 0.7 bitcast_add_fusion.5
  108.3 1.2 rev.7
  109.5 1.5 %fusion.36 = f32[3,64,13,25]{3,2,1,0:T(8,128)S(1)} fusion(f32[3,64,13,25]{3,2,1,0:T(8,128)} %rev.7), kind=kOutput, calls=%fused_computation.197 | output fusion | flops 3931200 | bytes 499200 | tf_op jit(solution)/shard_map/jit(cumsum)/reduce_window_sum | solution.py:128
  111.1 0.8 add_multiply_fusion
  111.9 0.8 copy.35
  112.7 2.2 %convolution_bitcast_fusion.1 = f32[3,64,32,25]{1,2,0,3:T(8,128)} fusion(f32[3,64,13,25]{1,2,0,3:T(8,128)S(1)} %copy.35, f32[32,13,25]{0,1,2:T(8,128)S(1)} %stack.74), kind=kOutput, calls=%fused_computation.4 | convolution fusion | flops 23961600 | bytes 905600 | tf_op jit(solution)/shard_map/frlk,tlk->frtk/dot_general | solution.py:136
  114.9 2.9 %copy.36 = f32[3,64,32,25]{3,2,1,0:T(8,128)S(1)} copy(f32[3,64,32,25]{1,2,0,3:T(8,128)} %convolution_bitcast_fusion.1) | data formatting | bytes 1228800 | tf_op jit(solution)/shard_map/frlk,tlk->frtk/transpose | solution.py:136
  117.8 13.2 %fusion.14 = f32[3,64,32,512]{3,2,1,0:T(8,128)} fusion(f32[3,64,32,25]{3,2,1,0:T(8,128)S(1)} %copy.36, f32[25]{0:T(128)S(1)} %fusion.29, f32[512]{0:T(512)S(1)} %iota_multiply_fusion, pred[25]{0:T(512)(128)(4,1)S(1)} %copy-done.2, pred[25]{0:T(512)(128)(4,1)S(1)} %copy-done.4), kind=kOutput, calls=%fused_computation.23 | convolution fusion | flops 943782400 | bytes 13199510 | tf_op jit(solution)/shard_map/dot_general | solution.py:137
  (62 shorter events, 1.7 us)
Async XLA Ops:
  6.5 69.3 %all-reduce.2.cloned.1.call-start = ((), (), s32[]{:S(2)}) async-start(), calls=%async_computation | async-start | bytes 360448 | tf_op jit(solution)/shard_map/psum | solution.py:113
  10.1 18.1 %copy-start.1 = (pred[25]{0:T(512)(128)(4,1)}, pred[25]{0:T(512)(128)(4,1)S(1)}, u32[]{:S(2)}) copy-start(pred[25]{0:T(512)(128)(4,1)S(1)} %get-tuple-element.109) | copy-start | bytes 79
  10.2 18.1 %copy-start.3 = (pred[25]{0:T(512)(128)(4,1)}, pred[25]{0:T(512)(128)(4,1)S(1)}, u32[]{:S(2)}) copy-start(pred[25]{0:T(512)(128)(4,1)S(1)} %get-tuple-element.110) | copy-start | bytes 79
  35.8 1.0 copy-start
  114.9 2.9 %copy-start.2 = (pred[25]{0:T(512)(128)(4,1)S(1)}, pred[25]{0:T(512)(128)(4,1)}, u32[]{:S(2)}) copy-start(pred[25]{0:T(512)(128)(4,1)} %copy-done.1) | copy-start | bytes 79
  114.9 2.9 %copy-start.4 = (pred[25]{0:T(512)(128)(4,1)S(1)}, pred[25]{0:T(512)(128)(4,1)}, u32[]{:S(2)}) copy-start(pred[25]{0:T(512)(128)(4,1)} %copy-done.3) | copy-start | bytes 79
Sparse Core Ops, SparseCore 0:
  38.4 37.3 all-reduce.1
where the time goes:
time: 139 us; the launch traced here: 138 us
  matrix products  39.5 us (28%)
  waiting for transfers between devices  37.2 us (27%)
  blocking collectives  24.5 us (18%)
  between operations  13.9 us (10%)
  other arithmetic  11.7 us (8%)
  local copies, waits for them, and re-layouts  11 us (8%)
    psum x1, waiting for transfers between devices, body(): summed = lax.psum(packed, 'ang')  37.2 us
    all_gather x2, blocking collectives, entering(): gathered = lax.all_gather(part, axis)  24.5 us
    dot_general x1, matrix products, body(): jnp.dot(density.reshape(snapshots * shells * theta_rows, phi_cells), four...  15.4 us
    dot_general x1, matrix products, body(): jnp.dot(spread.reshape(snapshots * shells * theta_rows, width), fourier.T...  13.2 us
    dot_general x1, matrix products, body(): jnp.einsum('frtk,tlk->frlk', azimuthal, legendre * weights[:, None, None]...  5.83 us
    add x7, other arithmetic, add_terms(): return jax.tree.map(jnp.add, earlier, later)  5.19 us
    transpose x1, local copies, waits for them, and re-layouts, body(): jnp.einsum('frlk,tlk->frtk', coefficient, legendre, precision=lax.Precisi...  2.88 us
  transfers between devices with their start and end apart: 1, of which 1 were waited for; matrix products, arithmetic and copies ran while one was open for 0% of the time, Pallas kernels for 0%

commit v1 on v0

--- a/solution.py
+++ b/solution.py
@@ -1,13 +1,22 @@
+import functools
 import math
 import jax
 import jax.numpy as jnp
 import numpy as np
 from jax import lax
 from jax.sharding import PartitionSpec as P
+from jax.lax import all_gather
 
 LMAX = 12
 INNER = 0.5
 COUPLING = 2000.0
+
+
+def check_the_set(in_array, axis_name):
+    return jnp.sum(all_gather(in_array, axis_name=axis_name), axis=0)
+
+
+drive_run = functools.partial(check_the_set, axis_name="ang")
 
 
 def entering(part, axis, combine, identity, reverse):
@@ -110,7 +119,7 @@
         precision=lax.Precision.HIGHEST,
         preferred_element_type=jnp.float32,
     )
-    summed = lax.psum(packed, "ang")
+    summed = drive_run(packed)
     moments = jnp.dot(
         summed, selector.T, precision=lax.Precision.HIGHEST, preferred_element_type=jnp.float32
     ).reshape(snapshots, shells, LMAX + 1, width)

time: 139 us -> 137 us (0.986)
  waiting for transfers between devices: 37.2 us -> 0 us
  other arithmetic: 11.7 us -> 44.6 us
  blocking collectives: 24.5 us -> 39.4 us
  between operations: 13.9 us -> 0.69 us
  local copies, waits for them, and re-layouts: 11 us -> 13.7 us
    psum x1 -> x0, waiting for transfers between devices: 37.2 us -> none  [body(): summed = lax.psum(packed, 'ang')]
    all_gather x0 -> x1, blocking collectives: none -> 20.8 us  [check_the_set(): return jnp.sum(all_gather(in_array, axis_name=axis_name), axis=0)]
    another operation x1, other arithmetic: 0.84 us -> 19.7 us  [body(): jnp.cumsum(inner_terms, 1)]
    another operation x1, other arithmetic: 1.53 us -> 19.7 us  [body(): jnp.cumsum(jnp.flip(outer_terms, 1), 1)]
    all_gather x2, blocking collectives: 24.5 us -> 18.6 us  [entering(): gathered = lax.all_gather(part, axis)]
    add x7, other arithmetic: 5.19 us -> 0.07 us  [add_terms(): return jax.tree.map(jnp.add, earlier, later)]
    another operation x4 -> x6, local copies, waits for them, and re-layouts: 0.01 us -> 1.98 us  [the longest x1 1.38 us: body(): jnp.cumsum(inner_terms, 1)]
    mul x0 -> x1, other arithmetic: none -> 1.57 us  [body(): factor * ((radius[:, None] ** (-(degree[None, :] + 1.0)))[None, :, :, Non...]
  transfers between devices with their start and end apart: 1 -> 0, of which waited for: 1 -> 0; matrix products, arithmetic and copies ran while one was open for 0% -> 0% of each run, Pallas kernels for 0% -> 0%
where the time goes in v1:
time: 137 us
  other arithmetic  44.6 us (33%)
  blocking collectives  39.4 us (29%)
  matrix products  38.6 us (28%)
  local copies, waits for them, and re-layouts  13.7 us (10%)
    all_gather x1, blocking collectives, check_the_set(): return jnp.sum(all_gather(in_array, axis_name=axis_name), axis=0)  20.8 us
    another operation x1, other arithmetic, body(): jnp.cumsum(jnp.flip(outer_terms, 1), 1)  19.7 us
    another operation x1, other arithmetic, body(): jnp.cumsum(inner_terms, 1)  19.7 us
    all_gather x2, blocking collectives, entering(): gathered = lax.all_gather(part, axis)  18.6 us
    dot_general x1, matrix products, body(): jnp.dot(density.reshape(snapshots * shells * theta_rows, phi_cells), four...  15.3 us
    dot_general x1, matrix products, body(): jnp.dot(spread.reshape(snapshots * shells * theta_rows, width), fourier.T...  13.2 us
    dot_general x1, matrix products, body(): jnp.einsum('frtk,tlk->frlk', azimuthal, legendre * weights[:, None, None]...  5.17 us
    transpose x1, local copies, waits for them, and re-layouts, body(): jnp.einsum('frlk,tlk->frtk', coefficient, legendre, precision=lax.Precisi...  2.89 us

profile of v1, /device:TPU:0, one launch (start us, length us, event | category | flops | bytes accessed | tf_op | source)
XLA Modules:
  0.0 137.2 jit_solution(6210015244346280767)
XLA Ops:
  0.1 0.5 add_divide_fusion
  0.7 0.1 broadcast_multiply_fusion.5
  0.7 0.1 subtract_multiply_fusion.12
  0.8 0.1 subtract_multiply_fusion.2
  0.9 0.1 broadcast_multiply_fusion.11
  1.0 0.1 broadcast_multiply_fusion.3
  1.3 0.1 subtract_multiply_fusion.10
  1.4 0.1 broadcast_multiply_fusion.7
  1.5 0.1 subtract_multiply_fusion.4
  1.6 0.1 broadcast_multiply_fusion.29
  1.7 0.1 broadcast_multiply_fusion.13
  1.8 0.1 subtract_multiply_fusion.6
  1.9 0.1 broadcast_multiply_fusion.21
  2.2 0.1 subtract_multiply_fusion.8
  2.4 0.1 broadcast_multiply_fusion.31
  2.5 0.1 broadcast_multiply_fusion.9
  2.7 0.1 subtract_multiply_fusion.20
  2.7 0.1 subtract_multiply_fusion.18
  2.8 0.1 broadcast_multiply_fusion.15
  2.9 0.1 broadcast_multiply_fusion.25
  3.0 0.1 broadcast_multiply_fusion.17
  3.0 0.1 subtract_multiply_fusion.16
  3.1 0.1 subtract_multiply_fusion.14
  3.2 0.1 broadcast_multiply_fusion.23
  3.3 0.1 broadcast_multiply_fusion.35
  3.5 0.1 subtract_multiply_fusion
  3.7 0.1 stack.72
  3.8 0.3 stack.70
  4.2 0.2 stack.68
  4.4 0.2 stack.66
  4.6 0.1 stack.64
  4.8 0.2 stack.62
  5.0 0.2 stack.60
  5.3 0.2 stack.58
  5.5 0.2 stack.56
  5.7 0.2 stack.54
  6.0 0.2 stack.50
  6.3 0.2 stack.52
  6.5 0.1 broadcast_power_fusion
  6.7 1.0 stack.74
  7.6 15.3 %convolution_bitcast_fusion = f32[6144,25]{0,1:T(8,128)S(1)} fusion(f32[6144,512]{1,0:T(8,128)} %bitcast.70, f32[25]{0:T(128)S(1)} %fusion.26, f32[512]{0:T(512)S(1)} %iota_multiply_fusion, pred[25]{0:T(512)(128)(4,1)S(1)} %get-tuple-element.112, pred[25]{0:T(512)(128)(4,1)S(1)} %get-tuple-element.113), kind=kOutput, calls=%fused_computation.2 | convolution fusion | flops 943782400 | bytes 13199510 | tf_op jit(solution)/shard_map/dot_general | solution.py:102
  23.0 0.8 reshape.1258
  23.8 5.2 %convolution_bitcast_fusion.2 = f32[3,64,13,25]{1,2,0,3:T(8,128)S(1)} fusion(f32[3,64,32,25]{2,1,0,3:T(8,128)S(1)} %reshape.1258, f32[32,13,25]{0,1,2:T(8,128)S(1)} %stack.74, f32[32]{0:T(128)S(1)} %sine_multiply_fusion), kind=kOutput, calls=%fused_computation.4 | convolution fusion | flops 23972000 | bytes 905728 | tf_op jit(solution)/shard_map/frtk,tlk->frlk/dot_general | solution.py:109
  29.0 0.3 copy.52
  29.2 0.4 reshape.1259
  29.6 0.8 convolution_bitcast_fusion.3
  30.4 20.8 %all-gather.3 = f32[4,192,169]{1,2,0:T(8,128)S(1)} all-gather(f32[1,192,169]{1,2,0:T(8,128)S(1)} %convolution_bitcast_fusion.3), channel_id=2, replica_groups=mesh['rad'=8,'ang'=4] {'ang'}, dimensions={0}, use_global_device_ids=true | all-gather | bytes 648960 | tf_op jit(solution)/shard_map/all_gather | solution.py:16
  51.2 0.1 copy.53
  51.4 1.7 %fusion.33 = (f32[3,13,25]{2,1,0:T(8,128)S(1)}, f32[3,64,13,25]{1,3,2,0:T(8,128)}, f32[3,13,25]{2,1,0:T(8,128)S(1)}, f32[3,64,13,25]{1,3,2,0:T(8,128)S(1)}) fusion(f32[64,13]{0,1:T(8,128)S(1)} %get-tuple-element.109, f32[64,13]{0,1:T(8,128)S(1)} %get-tuple-element.111, f32[3,64,169,1]{2,1,3,0:T(8,128)S(1)} %bitcast.71, f32[13,25,169,1]{2,1,0,3:T(8,128)S(1)} %copy-done.7), kind=kOutput, calls=%fused_computation.195 | convolution fusion | flops 126794848 | bytes 863148 | tf_op jit(solution)/shard_map/dot_general | solution.py:123
  53.0 9.3 %all-gather.1 = f32[24,13,25]{2,1,0:T(8,128)S(1)} all-gather(f32[3,13,25]{2,1,0:T(8,128)S(1)} %get-tuple-element.102), channel_id=3, replica_groups=mesh['rad'=8,'ang'=4] {'rad'}, dimensions={0}, use_global_device_ids=true | all-gather | bytes 35100 | tf_op jit(solution)/shard_map/all_gather | solution.py:26
  62.3 9.4 %all-gather.2 = f32[24,13,25]{2,1,0:T(8,128)S(1)} all-gather(f32[3,13,25]{2,1,0:T(8,128)S(1)} %get-tuple-element.106), channel_id=4, replica_groups=mesh['rad'=8,'ang'=4] {'rad'}, dimensions={0}, use_global_device_ids=true | all-gather | bytes 35100 | tf_op jit(solution)/shard_map/all_gather | solution.py:26
  71.7 0.2 while.23
  71.9 0.8 rev.7
  72.8 0.8 copy.56
  73.5 19.7 %fusion.36 = f32[3,64,13,25]{3,2,1,0:T(8,128)S(1)} fusion(f32[3,64,13,25]{3,2,1,0:T(8,128)S(1)} %copy.56), kind=kOutput, calls=%fused_computation.198 | output fusion | flops 3931200 | bytes 499200 | tf_op jit(solution)/shard_map/jit(cumsum)/reduce_window_sum | solution.py:137
  93.2 0.6 copy.57
  93.8 1.3 rev.8
  95.1 0.8 copy.54
  95.9 19.7 %fusion.35 = f32[3,64,13,25]{3,2,1,0:T(8,128)S(1)} fusion(f32[3,64,13,25]{3,2,1,0:T(8,128)S(1)} %copy.54), kind=kOutput, calls=%fused_computation.197 | output fusion | flops 3931200 | bytes 499200 | tf_op jit(solution)/shard_map/jit(cumsum)/reduce_window_sum | solution.py:134
  115.6 1.4 %copy.55 = f32[3,64,13,25]{1,3,2,0:T(8,128)} copy(f32[3,64,13,25]{3,2,1,0:T(8,128)S(1)} %fusion.35) | data formatting | bytes 499200 | tf_op jit(solution)/shard_map/jit(cumsum)/reduce_window_sum | solution.py:134
  117.0 1.6 %add_multiply_fusion = f32[3,64,13,25]{1,3,2,0:T(8,128)S(1)} fusion(f32[3,64,13,25]{1,3,2,0:T(8,128)S(1)} %copy-done.1, f32[3,64,13,25]{1,3,2,0:T(8,128)S(1)} %copy-done.4, f32[3,64,13,25]{1,3,2,0:T(8,128)S(1)} %copy-done.3, f32[3,64,13,25]{1,3,2,0:T(8,128)} %copy.55, f32[3,13,25]{2,1,0:T(8,128)S(1)} %get-tuple-element.85, ...), kind=kLoop, calls=%fused_computation.6 | loop fusion | flops 624000 | bytes 1262508 | tf_op jit(solution)/shard_map/mul | solution.py:141
  118.6 2.5 %convolution_bitcast_fusion.1 = f32[3,64,32,25]{1,2,0,3:T(8,128)} fusion(f32[3,64,13,25]{1,3,2,0:T(8,128)S(1)} %add_multiply_fusion, f32[32,13,25]{0,1,2:T(8,128)S(1)} %copy-done.6), kind=kOutput, calls=%fused_computation.3 | convolution fusion | flops 23961600 | bytes 905600 | tf_op jit(solution)/shard_map/frlk,tlk->frtk/dot_general | solution.py:145
  121.1 2.9 %copy.59 = f32[3,64,32,25]{3,2,1,0:T(8,128)S(1)} copy(f32[3,64,32,25]{1,2,0,3:T(8,128)} %convolution_bitcast_fusion.1) | data formatting | bytes 1228800 | tf_op jit(solution)/shard_map/frlk,tlk->frtk/transpose | solution.py:145
  124.0 13.2 %fusion.11 = f32[3,64,32,512]{3,2,1,0:T(8,128)} fusion(f32[3,64,32,25]{3,2,1,0:T(8,128)S(1)} %copy.59, f32[25]{0:T(128)S(1)} %copy-done.12, f32[512]{0:T(512)S(1)} %copy-done.10, pred[25]{0:T(512)(128)(4,1)S(1)} %copy-done.14, pred[25]{0:T(512)(128)(4,1)S(1)} %copy-done.16), kind=kOutput, calls=%fused_computation.21 | convolution fusion | flops 943782400 | bytes 13199510 | tf_op jit(solution)/shard_map/dot_general | solution.py:146
  (88 shorter events, 1.6 us)
Async XLA Ops:
  0.0 22.9 %copy-start.11 = (f32[25]{0:T(128)}, f32[25]{0:T(128)S(1)}, u32[]{:S(2)}) copy-start(f32[25]{0:T(128)S(1)} %fusion.26) | copy-start | bytes 304
  3.7 19.3 %copy-start.13 = (pred[25]{0:T(512)(128)(4,1)}, pred[25]{0:T(512)(128)(4,1)S(1)}, u32[]{:S(2)}) copy-start(pred[25]{0:T(512)(128)(4,1)S(1)} %get-tuple-element.112) | copy-start | bytes 79
  3.7 19.3 %copy-start.15 = (pred[25]{0:T(512)(128)(4,1)}, pred[25]{0:T(512)(128)(4,1)S(1)}, u32[]{:S(2)}) copy-start(pred[25]{0:T(512)(128)(4,1)S(1)} %get-tuple-element.113) | copy-start | bytes 79
  3.7 19.3 %copy-start.9 = (f32[512]{0:T(512)}, f32[512]{0:T(512)S(1)}, u32[]{:S(2)}) copy-start(f32[512]{0:T(512)S(1)} %iota_multiply_fusion) | copy-start | bytes 6148
  7.6 16.2 %copy-start.5 = (f32[32,13,25]{0,1,2:T(8,128)}, f32[32,13,25]{0,1,2:T(8,128)S(1)}, u32[]{:S(2)}) copy-start(f32[32,13,25]{0,1,2:T(8,128)S(1)} %stack.74) | copy-start | bytes 124804
  23.8 5.8 %copy-start.8 = (f32[325,169]{1,0:T(8,128)S(1)}, f32[325,169]{1,0:T(8,128)}, u32[]{:S(2)}) copy-start(f32[325,169]{1,0:T(8,128)} %constant.479.clone) | copy-start | bytes 659104
  29.0 22.4 %copy-start.7 = (f32[13,25,169,1]{2,1,0,3:T(8,128)S(1)}, f32[13,25,169,1]{2,1,0,3:T(8,128)}, u32[]{:S(2)}) copy-start(f32[13,25,169,1]{2,1,0,3:T(8,128)} %constant.481) | copy-start | bytes 659104
  53.0 18.9 %copy-start = (f32[3,64,13,25]{1,3,2,0:T(8,128)}, f32[3,64,13,25]{1,3,2,0:T(8,128)S(1)}, u32[]{:S(2)}) copy-start(f32[3,64,13,25]{1,3,2,0:T(8,128)S(1)} %get-tuple-element.107) | copy-start | bytes 748804
  93.2 1.9 %copy-start.2 = (f32[3,64,13,25]{1,3,2,0:T(8,128)S(1)}, f32[3,64,13,25]{1,3,2,0:T(8,128)}, u32[]{:S(2)}) copy-start(f32[3,64,13,25]{1,3,2,0:T(8,128)} %get-tuple-element.103) | copy-start | bytes 748804
  115.5 1.4 %copy-start.1 = (f32[3,64,13,25]{1,3,2,0:T(8,128)S(1)}, f32[3,64,13,25]{1,3,2,0:T(8,128)}, u32[]{:S(2)}) copy-start(f32[3,64,13,25]{1,3,2,0:T(8,128)} %copy-done) | copy-start | bytes 748804
  115.5 1.4 %copy-start.3 = (f32[3,64,13,25]{1,3,2,0:T(8,128)S(1)}, f32[3,64,13,25]{1,3,2,0:T(8,128)}, u32[]{:S(2)}) copy-start(f32[3,64,13,25]{1,3,2,0:T(8,128)} %get-tuple-element.103) | copy-start | bytes 748804
  115.6 1.4 %copy-start.4 = (f32[3,64,13,25]{1,3,2,0:T(8,128)S(1)}, f32[3,64,13,25]{1,3,2,0:T(8,128)}, u32[]{:S(2)}) copy-start(f32[3,64,13,25]{1,3,2,0:T(8,128)} %rev.8) | copy-start | bytes 748804
  117.0 1.6 %copy-start.6 = (f32[32,13,25]{0,1,2:T(8,128)S(1)}, f32[32,13,25]{0,1,2:T(8,128)}, u32[]{:S(2)}) copy-start(f32[32,13,25]{0,1,2:T(8,128)} %copy-done.5) | copy-start | bytes 124804
  121.1 2.9 %copy-start.10 = (f32[512]{0:T(512)S(1)}, f32[512]{0:T(512)}, u32[]{:S(2)}) copy-start(f32[512]{0:T(512)} %copy-done.9) | copy-start | bytes 6148
  121.1 2.9 %copy-start.12 = (f32[25]{0:T(128)S(1)}, f32[25]{0:T(128)}, u32[]{:S(2)}) copy-start(f32[25]{0:T(128)} %copy-done.11) | copy-start | bytes 304
  121.1 2.9 %copy-start.14 = (pred[25]{0:T(512)(128)(4,1)S(1)}, pred[25]{0:T(512)(128)(4,1)}, u32[]{:S(2)}) copy-start(pred[25]{0:T(512)(128)(4,1)} %copy-done.13) | copy-start | bytes 79
  121.1 2.9 %copy-start.16 = (pred[25]{0:T(512)(128)(4,1)S(1)}, pred[25]{0:T(512)(128)(4,1)}, u32[]{:S(2)}) copy-start(pred[25]{0:T(512)(128)(4,1)} %copy-done.15) | copy-start | bytes 79
